TPU v7x, 32 devices: a 4x2x2 block of a 4x4x8 slice. The times are simulated.
32 devices in a mesh: dp: 4 (over y, z), pp: 8 (over x, core).
Axes of the slice: x: 4, y: 2, z: 2, core: 2. Of those that a mesh axis runs over, the one named last changes fastest.
The devices are a block of a 4x4x8 slice.
Arguments:
- x_in: bfloat16 [4, 16, 128, 1536], P('dp'), parts along dimension 0
- cond_vec: bfloat16 [4, 1536], P('dp'), parts along dimension 0
- pos_ids: int32 [16, 128, 3], replicated
- w_mod: bfloat16 [8, 1536, 4608], P('pp')
- b_mod: bfloat16 [8, 4608], P('pp')
- w_one: bfloat16 [8, 1536, 10752], P('pp')
- b_one: bfloat16 [8, 10752], P('pp')
- qk_scale: bfloat16 [8, 2, 64], P('pp')
- w_two: bfloat16 [8, 7680, 1536], P('pp')
- b_two: bfloat16 [8, 1536], P('pp')
- k_prev: bfloat16 [8, 4, 16, 128, 1536], P('pp', 'dp'), parts along dimension 1
- v_prev: bfloat16 [8, 4, 16, 128, 1536], P('pp', 'dp'), parts along dimension 1
Outputs:
- output 1: bfloat16 [4, 16, 128, 1536], P('dp', 'pp'), parts along dimension 0
- output 2: bfloat16 [8, 4, 16, 128, 1536], P('pp', 'dp'), parts along dimension 1
- output 3: bfloat16 [8, 4, 16, 128, 1536], P('pp', 'dp'), parts along dimension 1
There are 4 independent parts. A program takes and returns all parts, laid end to end along the dimension named above; an argument that names none is the same for every part.
All inputs are finite; a program needn't handle non-finite values.
Results may differ from a plain program's by a relative error of at most 0.0148771.
Values are sent between devices in bfloat16 or wider.
A program may use at most 768 MiB of HBM per device.

v0:
```python
import math
import jax
import jax.numpy as jnp
from jax import lax
from jax.sharding import PartitionSpec as P


def layer_norm(hidden):
    act32 = hidden.astype(jnp.float32)
    centered = act32 - jnp.mean(act32, axis=-1, keepdims=True)
    return centered * lax.rsqrt(jnp.mean(centered * centered, axis=-1, keepdims=True) + 1e-6)


def rope_tables(pos_ids, head_dim):
    axis_zero = head_dim // 8
    axis_rest = (head_dim - axis_zero) // 2
    pieces = []
    for axis_idx, axis_dim in enumerate((axis_zero, axis_rest, head_dim - axis_zero - axis_rest)):
        axis_freqs = 1.0 / (10000.0 ** (jnp.arange(0, axis_dim, 2, dtype=jnp.float32) / axis_dim))
        pieces.append(pos_ids[..., axis_idx:axis_idx + 1].astype(jnp.float32) * axis_freqs)
    angles = jnp.concatenate(pieces, axis=-1)[..., None, :]
    return jnp.cos(angles), jnp.sin(angles)


def rms_rope(raw_heads, norm_gain, cos_tab, sin_tab):
    raw32 = raw_heads.astype(jnp.float32)
    normed = raw32 * lax.rsqrt(jnp.mean(raw32 * raw32, axis=-1, keepdims=True) + 1e-6) * norm_gain.astype(jnp.float32)
    pair_view = normed.reshape(normed.shape[:-1] + (normed.shape[-1] // 2, 2))
    even_part = pair_view[..., 0]
    odd_part = pair_view[..., 1]
    rotated = jnp.stack([cos_tab * even_part - sin_tab * odd_part, sin_tab * even_part + cos_tab * odd_part], axis=-1)
    return rotated.reshape(raw_heads.shape).astype(jnp.bfloat16)


def solution(mesh):
    stages = mesh.shape['pp']
    send_pairs = [(src_stage, src_stage + 1) for src_stage in range(stages - 1)]

    def stage_program(x_in, cond_vec, pos_ids, w_mod, b_mod, w_one, b_one, qk_scale, w_two, b_two, k_prev, v_prev):
        batch_size, patches, patch_tok, width = x_in.shape
        stage_layers = w_one.shape[0]
        head_dim = qk_scale.shape[-1]
        head_count = width // head_dim
        seq_len = patches * patch_tok
        score_scale = 1.0 / math.sqrt(head_dim)
        head_shape = (batch_size, patch_tok, head_count, head_dim)
        stage_idx = lax.axis_index('pp')
        cond_act = jax.nn.silu(cond_vec.astype(jnp.float32)).astype(jnp.bfloat16)
        mod_all = jnp.einsum('bd,lde->lbe', cond_act, w_mod, preferred_element_type=jnp.float32) + b_mod[:, None, :].astype(jnp.float32)
        cos_all, sin_all = rope_tables(pos_ids, head_dim)

        def run_patch(hidden, patch_idx, k_buf, v_buf):
            cos_tab = lax.dynamic_index_in_dim(cos_all, patch_idx, axis=0, keepdims=False)
            sin_tab = lax.dynamic_index_in_dim(sin_all, patch_idx, axis=0, keepdims=False)
            for layer_idx in range(stage_layers):
                mod_vals = mod_all[layer_idx][:, None, :]
                shift_mod = mod_vals[..., :width]
                scale_mod = mod_vals[..., width:2 * width]
                gate_mod = mod_vals[..., 2 * width:]
                h_mod = (layer_norm(hidden) * (1.0 + scale_mod) + shift_mod).astype(jnp.bfloat16)
                proj_out = (jnp.einsum('btd,de->bte', h_mod, w_one[layer_idx], preferred_element_type=jnp.float32) + b_one[layer_idx].astype(jnp.float32)).astype(jnp.bfloat16)
                q_rot = rms_rope(proj_out[..., :width].reshape(head_shape), qk_scale[layer_idx, 0], cos_tab, sin_tab)
                k_rot = rms_rope(proj_out[..., width:2 * width].reshape(head_shape), qk_scale[layer_idx, 1], cos_tab, sin_tab)
                v_fresh = proj_out[..., 2 * width:3 * width]
                k_buf = lax.dynamic_update_slice(k_buf, k_rot.reshape(1, batch_size, 1, patch_tok, width), (layer_idx, 0, patch_idx, 0, 0))
                v_buf = lax.dynamic_update_slice(v_buf, v_fresh.reshape(1, batch_size, 1, patch_tok, width), (layer_idx, 0, patch_idx, 0, 0))
                key_all = k_buf[layer_idx].reshape(batch_size, seq_len, head_count, head_dim)
                val_all = v_buf[layer_idx].reshape(batch_size, seq_len, head_count, head_dim)
                scores = jnp.einsum('bqhd,bkhd->bhqk', q_rot, key_all, preferred_element_type=jnp.float32) * score_scale
                prob_bf = jax.nn.softmax(scores, axis=-1).astype(jnp.bfloat16)
                attn_out = jnp.einsum('bhqk,bkhd->bqhd', prob_bf, val_all, preferred_element_type=jnp.float32).astype(jnp.bfloat16).reshape(batch_size, patch_tok, width)
                mlp_act = jax.nn.gelu(proj_out[..., 3 * width:].astype(jnp.float32), approximate=True).astype(jnp.bfloat16)
                joined = jnp.concatenate([attn_out, mlp_act], axis=-1)
                block_out = jnp.einsum('bte,ed->btd', joined, w_two[layer_idx], preferred_element_type=jnp.float32) + b_two[layer_idx].astype(jnp.float32)
                hidden = (hidden.astype(jnp.float32) + gate_mod * block_out).astype(jnp.bfloat16)
            return hidden, k_buf, v_buf

        def skip_patch(hidden, patch_idx, k_buf, v_buf):
            return hidden, k_buf, v_buf

        def step_body(step_idx, loop_carry):
            recv_act, k_buf, v_buf, out_acc = loop_carry
            patch_idx = step_idx - stage_idx
            is_valid = (patch_idx >= 0) & (patch_idx < patches)
            safe_idx = jnp.clip(patch_idx, 0, patches - 1)
            first_in = lax.dynamic_index_in_dim(x_in, safe_idx, axis=1, keepdims=False)
            hidden = jnp.where(stage_idx == 0, first_in, recv_act)
            hidden, k_buf, v_buf = lax.cond(is_valid, run_patch, skip_patch, hidden, safe_idx, k_buf, v_buf)
            old_slot = lax.dynamic_index_in_dim(out_acc, safe_idx, axis=1, keepdims=False)
            new_slot = jnp.where(is_valid & (stage_idx == stages - 1), hidden, old_slot)
            out_acc = lax.dynamic_update_index_in_dim(out_acc, new_slot, safe_idx, axis=1)
            recv_act = lax.ppermute(hidden, 'pp', send_pairs)
            return recv_act, k_buf, v_buf, out_acc

        init_carry = (jnp.zeros((batch_size, patch_tok, width), jnp.bfloat16), k_prev, v_prev, jnp.zeros_like(x_in))
        recv_act, k_new, v_new, out_acc = lax.fori_loop(0, patches + stages - 1, step_body, init_carry)
        last_only = jnp.where(stage_idx == stages - 1, out_acc, jnp.zeros_like(out_acc))
        x_out = lax.psum_scatter(last_only, 'pp', scatter_dimension=1, tiled=True)
        return x_out, k_new, v_new

    return jax.shard_map(
        stage_program, mesh=mesh,
        in_specs=(P('dp'), P('dp'), P(), P('pp'), P('pp'), P('pp'), P('pp'), P('pp'), P('pp'), P('pp'), P('pp', 'dp'), P('pp', 'dp')),
        out_specs=(P('dp', 'pp'), P('pp', 'dp'), P('pp', 'dp')),
        check_vma=False)
```

profile of v0, /device:TPU:81, one launch (start us, length us, event | category | flops | bytes accessed | tf_op | source)
XLA Modules:
  0.0 3990.7 jit_solution(7465287083346361806)
XLA Ops:
  39.6 3426.7 %while.20 = (s32[]{:T(128)}, bf16[1,128,1536]{2,1,0:T(8,128)(2,1)}, bf16[1,1,16,128,1536]{3,2,4,1,0:T(8,128)(2,1)}, bf16[1,1,16,128,1536]{3,2,4,1,0:T(8,128)(2,1...) while((s32[]{:T(128)}, bf16[1,128,1536]{2,1,0:T(8,128)(2,1)}, ...), condition=%wide.region_9.10_spmd, body=%wide.region_0.9_spmd.sunk | while | flops 8913836032 | bytes 184911664 | solution.py:96
  47.3 158.4 %collective-permute-done = bf16[1,128,1536]{2,1,0:T(8,128)(2,1)} collective-permute-done((bf16[1,128,1536]{2,1,0:T(8,128)(2,1)S(1)}, bf16[1,128,1536]{2,1,0:T(8,128)(2,1)}, u32[]{:S(2)}, u32[]{:S(2)}) %collective-permute-start) | collective-permute-done | bytes 393248 | tf_op jit(solution)/shard_map/while/body/eval_jaxpr/ppermute | solution.py:92
  206.8 160.5 %conditional.2 = ((bf16[1,128,1536]{2,1,0:T(8,128)(2,1)S(1)}, bf16[1,1,16,128,1536]{3,2,4,1,0:T(8,128)(2,1)}, bf16[1,1,16,128,1536]{3,2,4,1,0:T(8,128)(2,1)})) conditional(s32[]{:T(128)} %convert_element_type.272, (bf16[1,128,1536]{2,1,0:T(8,128)(2,1)S(1)}, bf16[1,1,16,128,1536]{3,2,4,1,0:T(8,128)(2,1)}, ...), branch_computations={%region_1.1_spmd, %region_2.8_spmd} | conditional | flops 8913442816 | bytes 180192160 | solution.py:88
  209.5 15.0 fusion.14
  259.7 20.8 dynamic_update_slice.13
  309.7 20.8 dynamic_update_slice.12
  375.1 160.5 %conditional.2 = ((bf16[1,128,1536]{2,1,0:T(8,128)(2,1)S(1)}, bf16[1,1,16,128,1536]{3,2,4,1,0:T(8,128)(2,1)}, bf16[1,1,16,128,1536]{3,2,4,1,0:T(8,128)(2,1)})) conditional(s32[]{:T(128)} %convert_element_type.272, (bf16[1,128,1536]{2,1,0:T(8,128)(2,1)S(1)}, bf16[1,1,16,128,1536]{3,2,4,1,0:T(8,128)(2,1)}, ...), branch_computations={%region_1.1_spmd, %region_2.8_spmd} | conditional | flops 8913442816 | bytes 180192160 | solution.py:88
  377.8 15.0 fusion.14
  428.0 20.8 dynamic_update_slice.13
  478.0 20.8 dynamic_update_slice.12
  546.0 160.5 %conditional.2 = ((bf16[1,128,1536]{2,1,0:T(8,128)(2,1)S(1)}, bf16[1,1,16,128,1536]{3,2,4,1,0:T(8,128)(2,1)}, bf16[1,1,16,128,1536]{3,2,4,1,0:T(8,128)(2,1)})) conditional(s32[]{:T(128)} %convert_element_type.272, (bf16[1,128,1536]{2,1,0:T(8,128)(2,1)S(1)}, bf16[1,1,16,128,1536]{3,2,4,1,0:T(8,128)(2,1)}, ...), branch_computations={%region_1.1_spmd, %region_2.8_spmd} | conditional | flops 8913442816 | bytes 180192160 | solution.py:88
  548.7 15.0 fusion.14
  598.8 20.8 dynamic_update_slice.13
  648.9 20.8 dynamic_update_slice.12
  716.8 160.5 %conditional.2 = ((bf16[1,128,1536]{2,1,0:T(8,128)(2,1)S(1)}, bf16[1,1,16,128,1536]{3,2,4,1,0:T(8,128)(2,1)}, bf16[1,1,16,128,1536]{3,2,4,1,0:T(8,128)(2,1)})) conditional(s32[]{:T(128)} %convert_element_type.272, (bf16[1,128,1536]{2,1,0:T(8,128)(2,1)S(1)}, bf16[1,1,16,128,1536]{3,2,4,1,0:T(8,128)(2,1)}, ...), branch_computations={%region_1.1_spmd, %region_2.8_spmd} | conditional | flops 8913442816 | bytes 180192160 | solution.py:88
  719.5 15.0 fusion.14
  769.6 20.8 dynamic_update_slice.13
  819.7 20.8 dynamic_update_slice.12
  887.6 160.5 %conditional.2 = ((bf16[1,128,1536]{2,1,0:T(8,128)(2,1)S(1)}, bf16[1,1,16,128,1536]{3,2,4,1,0:T(8,128)(2,1)}, bf16[1,1,16,128,1536]{3,2,4,1,0:T(8,128)(2,1)})) conditional(s32[]{:T(128)} %convert_element_type.272, (bf16[1,128,1536]{2,1,0:T(8,128)(2,1)S(1)}, bf16[1,1,16,128,1536]{3,2,4,1,0:T(8,128)(2,1)}, ...), branch_computations={%region_1.1_spmd, %region_2.8_spmd} | conditional | flops 8913442816 | bytes 180192160 | solution.py:88
  890.3 15.0 fusion.14
  940.4 20.8 dynamic_update_slice.13
  990.5 20.8 dynamic_update_slice.12
  1058.4 160.5 %conditional.2 = ((bf16[1,128,1536]{2,1,0:T(8,128)(2,1)S(1)}, bf16[1,1,16,128,1536]{3,2,4,1,0:T(8,128)(2,1)}, bf16[1,1,16,128,1536]{3,2,4,1,0:T(8,128)(2,1)})) conditional(s32[]{:T(128)} %convert_element_type.272, (bf16[1,128,1536]{2,1,0:T(8,128)(2,1)S(1)}, bf16[1,1,16,128,1536]{3,2,4,1,0:T(8,128)(2,1)}, ...), branch_computations={%region_1.1_spmd, %region_2.8_spmd} | conditional | flops 8913442816 | bytes 180192160 | solution.py:88
  1111.3 20.8 dynamic_update_slice.13
  1161.3 20.8 dynamic_update_slice.12
  1229.2 160.5 %conditional.2 = ((bf16[1,128,1536]{2,1,0:T(8,128)(2,1)S(1)}, bf16[1,1,16,128,1536]{3,2,4,1,0:T(8,128)(2,1)}, bf16[1,1,16,128,1536]{3,2,4,1,0:T(8,128)(2,1)})) conditional(s32[]{:T(128)} %convert_element_type.272, (bf16[1,128,1536]{2,1,0:T(8,128)(2,1)S(1)}, bf16[1,1,16,128,1536]{3,2,4,1,0:T(8,128)(2,1)}, ...), branch_computations={%region_1.1_spmd, %region_2.8_spmd} | conditional | flops 8913442816 | bytes 180192160 | solution.py:88
  1282.1 20.8 dynamic_update_slice.13
  1332.1 20.8 dynamic_update_slice.12
  1400.1 160.5 %conditional.2 = ((bf16[1,128,1536]{2,1,0:T(8,128)(2,1)S(1)}, bf16[1,1,16,128,1536]{3,2,4,1,0:T(8,128)(2,1)}, bf16[1,1,16,128,1536]{3,2,4,1,0:T(8,128)(2,1)})) conditional(s32[]{:T(128)} %convert_element_type.272, (bf16[1,128,1536]{2,1,0:T(8,128)(2,1)S(1)}, bf16[1,1,16,128,1536]{3,2,4,1,0:T(8,128)(2,1)}, ...), branch_computations={%region_1.1_spmd, %region_2.8_spmd} | conditional | flops 8913442816 | bytes 180192160 | solution.py:88
  1402.7 15.0 fusion.14
  1452.9 20.8 dynamic_update_slice.13
  1502.9 20.8 dynamic_update_slice.12
  1570.9 160.5 %conditional.2 = ((bf16[1,128,1536]{2,1,0:T(8,128)(2,1)S(1)}, bf16[1,1,16,128,1536]{3,2,4,1,0:T(8,128)(2,1)}, bf16[1,1,16,128,1536]{3,2,4,1,0:T(8,128)(2,1)})) conditional(s32[]{:T(128)} %convert_element_type.272, (bf16[1,128,1536]{2,1,0:T(8,128)(2,1)S(1)}, bf16[1,1,16,128,1536]{3,2,4,1,0:T(8,128)(2,1)}, ...), branch_computations={%region_1.1_spmd, %region_2.8_spmd} | conditional | flops 8913442816 | bytes 180192160 | solution.py:88
  1623.7 20.8 dynamic_update_slice.13
  1673.8 20.8 dynamic_update_slice.12
  1741.7 160.5 %conditional.2 = ((bf16[1,128,1536]{2,1,0:T(8,128)(2,1)S(1)}, bf16[1,1,16,128,1536]{3,2,4,1,0:T(8,128)(2,1)}, bf16[1,1,16,128,1536]{3,2,4,1,0:T(8,128)(2,1)})) conditional(s32[]{:T(128)} %convert_element_type.272, (bf16[1,128,1536]{2,1,0:T(8,128)(2,1)S(1)}, bf16[1,1,16,128,1536]{3,2,4,1,0:T(8,128)(2,1)}, ...), branch_computations={%region_1.1_spmd, %region_2.8_spmd} | conditional | flops 8913442816 | bytes 180192160 | solution.py:88
  1794.5 20.8 dynamic_update_slice.13
  1844.6 20.8 dynamic_update_slice.12
  1912.5 160.5 %conditional.2 = ((bf16[1,128,1536]{2,1,0:T(8,128)(2,1)S(1)}, bf16[1,1,16,128,1536]{3,2,4,1,0:T(8,128)(2,1)}, bf16[1,1,16,128,1536]{3,2,4,1,0:T(8,128)(2,1)})) conditional(s32[]{:T(128)} %convert_element_type.272, (bf16[1,128,1536]{2,1,0:T(8,128)(2,1)S(1)}, bf16[1,1,16,128,1536]{3,2,4,1,0:T(8,128)(2,1)}, ...), branch_computations={%region_1.1_spmd, %region_2.8_spmd} | conditional | flops 8913442816 | bytes 180192160 | solution.py:88
  1965.4 20.8 dynamic_update_slice.13
  2015.4 20.8 dynamic_update_slice.12
  2083.3 160.5 %conditional.2 = ((bf16[1,128,1536]{2,1,0:T(8,128)(2,1)S(1)}, bf16[1,1,16,128,1536]{3,2,4,1,0:T(8,128)(2,1)}, bf16[1,1,16,128,1536]{3,2,4,1,0:T(8,128)(2,1)})) conditional(s32[]{:T(128)} %convert_element_type.272, (bf16[1,128,1536]{2,1,0:T(8,128)(2,1)S(1)}, bf16[1,1,16,128,1536]{3,2,4,1,0:T(8,128)(2,1)}, ...), branch_computations={%region_1.1_spmd, %region_2.8_spmd} | conditional | flops 8913442816 | bytes 180192160 | solution.py:88
  2086.0 15.0 fusion.14
  2136.2 20.8 dynamic_update_slice.13
  2186.2 20.8 dynamic_update_slice.12
  2254.1 160.5 %conditional.2 = ((bf16[1,128,1536]{2,1,0:T(8,128)(2,1)S(1)}, bf16[1,1,16,128,1536]{3,2,4,1,0:T(8,128)(2,1)}, bf16[1,1,16,128,1536]{3,2,4,1,0:T(8,128)(2,1)})) conditional(s32[]{:T(128)} %convert_element_type.272, (bf16[1,128,1536]{2,1,0:T(8,128)(2,1)S(1)}, bf16[1,1,16,128,1536]{3,2,4,1,0:T(8,128)(2,1)}, ...), branch_computations={%region_1.1_spmd, %region_2.8_spmd} | conditional | flops 8913442816 | bytes 180192160 | solution.py:88
  2256.8 15.0 fusion.14
  2307.0 20.8 dynamic_update_slice.13
  2357.0 20.8 dynamic_update_slice.12
  2424.9 160.5 %conditional.2 = ((bf16[1,128,1536]{2,1,0:T(8,128)(2,1)S(1)}, bf16[1,1,16,128,1536]{3,2,4,1,0:T(8,128)(2,1)}, bf16[1,1,16,128,1536]{3,2,4,1,0:T(8,128)(2,1)})) conditional(s32[]{:T(128)} %convert_element_type.272, (bf16[1,128,1536]{2,1,0:T(8,128)(2,1)S(1)}, bf16[1,1,16,128,1536]{3,2,4,1,0:T(8,128)(2,1)}, ...), branch_computations={%region_1.1_spmd, %region_2.8_spmd} | conditional | flops 8913442816 | bytes 180192160 | solution.py:88
  2477.8 20.8 dynamic_update_slice.13
  2527.8 20.8 dynamic_update_slice.12
  2595.7 160.5 %conditional.2 = ((bf16[1,128,1536]{2,1,0:T(8,128)(2,1)S(1)}, bf16[1,1,16,128,1536]{3,2,4,1,0:T(8,128)(2,1)}, bf16[1,1,16,128,1536]{3,2,4,1,0:T(8,128)(2,1)})) conditional(s32[]{:T(128)} %convert_element_type.272, (bf16[1,128,1536]{2,1,0:T(8,128)(2,1)S(1)}, bf16[1,1,16,128,1536]{3,2,4,1,0:T(8,128)(2,1)}, ...), branch_computations={%region_1.1_spmd, %region_2.8_spmd} | conditional | flops 8913442816 | bytes 180192160 | solution.py:88
  2598.4 15.0 fusion.14
  2648.6 20.8 dynamic_update_slice.13
  2698.6 20.8 dynamic_update_slice.12
  2766.6 160.5 %conditional.2 = ((bf16[1,128,1536]{2,1,0:T(8,128)(2,1)S(1)}, bf16[1,1,16,128,1536]{3,2,4,1,0:T(8,128)(2,1)}, bf16[1,1,16,128,1536]{3,2,4,1,0:T(8,128)(2,1)})) conditional(s32[]{:T(128)} %convert_element_type.272, (bf16[1,128,1536]{2,1,0:T(8,128)(2,1)S(1)}, bf16[1,1,16,128,1536]{3,2,4,1,0:T(8,128)(2,1)}, ...), branch_computations={%region_1.1_spmd, %region_2.8_spmd} | conditional | flops 8913442816 | bytes 180192160 | solution.py:88
  2769.2 15.0 fusion.14
  2819.4 20.8 dynamic_update_slice.13
  2869.4 20.8 dynamic_update_slice.12
  2937.4 164.9 %collective-permute-start = (bf16[1,128,1536]{2,1,0:T(8,128)(2,1)S(1)}, bf16[1,128,1536]{2,1,0:T(8,128)(2,1)}, u32[]{:S(2)}, u32[]{:S(2)}) collective-permute-start(bf16[1,128,1536]{2,1,0:T(8,128)(2,1)S(1)} %get-tuple-element.604), channel_id=1, source_target_pairs={{0,1},{1,2},{2,3},{3,4},{4,5},{5,6},{6,7},{8,9},{9,10},{10,11},{11... | collective-permute-start | bytes 1179656 | tf_op jit(solution)/shard_map/while/body/eval_jaxpr/ppermute | solution.py:92
  3118.5 154.1 %collective-permute-start = (bf16[1,128,1536]{2,1,0:T(8,128)(2,1)S(1)}, bf16[1,128,1536]{2,1,0:T(8,128)(2,1)}, u32[]{:S(2)}, u32[]{:S(2)}) collective-permute-start(bf16[1,128,1536]{2,1,0:T(8,128)(2,1)S(1)} %get-tuple-element.604), channel_id=1, source_target_pairs={{0,1},{1,2},{2,3},{3,4},{4,5},{5,6},{6,7},{8,9},{9,10},{10,11},{11... | collective-permute-start | bytes 1179656 | tf_op jit(solution)/shard_map/while/body/eval_jaxpr/ppermute | solution.py:92
  3288.8 162.5 %collective-permute-start = (bf16[1,128,1536]{2,1,0:T(8,128)(2,1)S(1)}, bf16[1,128,1536]{2,1,0:T(8,128)(2,1)}, u32[]{:S(2)}, u32[]{:S(2)}) collective-permute-start(bf16[1,128,1536]{2,1,0:T(8,128)(2,1)S(1)} %get-tuple-element.604), channel_id=1, source_target_pairs={{0,1},{1,2},{2,3},{3,4},{4,5},{5,6},{6,7},{8,9},{9,10},{10,11},{11... | collective-permute-start | bytes 1179656 | tf_op jit(solution)/shard_map/while/body/eval_jaxpr/ppermute | solution.py:92
  3487.1 496.7 %reduce-scatter.2.cloned.1.call-done = bf16[1,2,128,1536]{3,2,1,0:T(8,128)(2,1)} async-done(((bf16[1,16,128,1536]{3,2,1,0:T(8,128)(2,1)}), bf16[1,2,128,1536]{3,2,1,0:T(8,128)(2,1)}) %reduce-scatter.2.cloned.1.call-update) | async-done | bytes 786448 | tf_op jit(solution)/shard_map/reduce_scatter | solution.py:98
  (787 shorter events, 2023.3 us)
Async XLA Ops:
  7.2 3976.6 %reduce-scatter.2.cloned.1.call-start = ((), (), s32[]{:S(2)}) async-start(), calls=%async_computation.1 | async-start | bytes 7077888 | tf_op jit(solution)/shard_map/reduce_scatter | solution.py:98
  40.8 164.9 %collective-permute-start = (bf16[1,128,1536]{2,1,0:T(8,128)(2,1)S(1)}, bf16[1,128,1536]{2,1,0:T(8,128)(2,1)}, u32[]{:S(2)}, u32[]{:S(2)}) collective-permute-start(bf16[1,128,1536]{2,1,0:T(8,128)(2,1)S(1)} %get-tuple-element.604), channel_id=1, source_target_pairs={{0,1},{1,2},{2,3},{3,4},{4,5},{5,6},{6,7},{8,9},{9,10},{10,11},{11... | collective-permute-start | bytes 1179656 | tf_op jit(solution)/shard_map/while/body/eval_jaxpr/ppermute | solution.py:92
  340.8 15.4 copy-start.1
  340.8 15.5 copy-start
  367.3 6.6 collective-permute-start
  509.1 15.4 copy-start.1
  509.1 15.5 copy-start
  535.7 9.1 collective-permute-start
  669.6 10.3 copy-start.4
  680.0 15.4 copy-start.1
  680.0 15.5 copy-start
  706.5 9.1 collective-permute-start
  850.8 15.4 copy-start.1
  850.8 15.5 copy-start
  877.3 9.1 collective-permute-start
  1011.3 10.3 copy-start.4
  1021.6 15.4 copy-start.1
  1021.6 15.5 copy-start
  1048.1 9.1 collective-permute-start
  1182.1 10.3 copy-start.4
  1192.4 15.4 copy-start.1
  1192.4 15.5 copy-start
  1219.0 9.1 collective-permute-start
  1363.2 15.4 copy-start.1
  1363.2 15.5 copy-start
  1389.8 9.1 collective-permute-start
  1523.7 10.3 copy-start.4
  1534.0 15.4 copy-start.1
  1534.0 15.5 copy-start
  1560.6 9.1 collective-permute-start
  1694.5 10.3 copy-start.4
  1704.9 15.4 copy-start.1
  1704.9 15.5 copy-start
  1731.4 9.1 collective-permute-start
  1875.7 15.4 copy-start.1
  1875.7 15.5 copy-start
  1902.2 9.1 collective-permute-start
  2036.2 10.3 copy-start.4
  2046.5 15.4 copy-start.1
  2046.5 15.5 copy-start
  2073.0 9.1 collective-permute-start
  2217.3 15.4 copy-start.1
  2217.3 15.5 copy-start
  2243.8 9.1 collective-permute-start
  2377.8 10.3 copy-start.4
  2388.1 15.4 copy-start.1
  2388.1 15.5 copy-start
  2414.6 9.1 collective-permute-start
  2548.6 10.3 copy-start.4
  2558.9 15.4 copy-start.1
  2558.9 15.5 copy-start
  2585.5 9.1 collective-permute-start
  2729.7 15.4 copy-start.1
  2729.7 15.5 copy-start
  2756.3 9.1 collective-permute-start
  2900.5 15.4 copy-start.1
  2900.5 15.5 copy-start
  2927.1 9.1 collective-permute-start
  2937.4 169.6 %collective-permute-start = (bf16[1,128,1536]{2,1,0:T(8,128)(2,1)S(1)}, bf16[1,128,1536]{2,1,0:T(8,128)(2,1)}, u32[]{:S(2)}, u32[]{:S(2)}) collective-permute-start(bf16[1,128,1536]{2,1,0:T(8,128)(2,1)S(1)} %get-tuple-element.604), channel_id=1, source_target_pairs={{0,1},{1,2},{2,3},{3,4},{4,5},{5,6},{6,7},{8,9},{9,10},{10,11},{11... | collective-permute-start | bytes 1179656 | tf_op jit(solution)/shard_map/while/body/eval_jaxpr/ppermute | solution.py:92
  3108.2 9.1 collective-permute-start
  3118.5 158.8 %collective-permute-start = (bf16[1,128,1536]{2,1,0:T(8,128)(2,1)S(1)}, bf16[1,128,1536]{2,1,0:T(8,128)(2,1)}, u32[]{:S(2)}, u32[]{:S(2)}) collective-permute-start(bf16[1,128,1536]{2,1,0:T(8,128)(2,1)S(1)} %get-tuple-element.604), channel_id=1, source_target_pairs={{0,1},{1,2},{2,3},{3,4},{4,5},{5,6},{6,7},{8,9},{9,10},{10,11},{11... | collective-permute-start | bytes 1179656 | tf_op jit(solution)/shard_map/while/body/eval_jaxpr/ppermute | solution.py:92
  3278.5 9.1 collective-permute-start
  3288.8 167.2 %collective-permute-start = (bf16[1,128,1536]{2,1,0:T(8,128)(2,1)S(1)}, bf16[1,128,1536]{2,1,0:T(8,128)(2,1)}, u32[]{:S(2)}, u32[]{:S(2)}) collective-permute-start(bf16[1,128,1536]{2,1,0:T(8,128)(2,1)S(1)} %get-tuple-element.604), channel_id=1, source_target_pairs={{0,1},{1,2},{2,3},{3,4},{4,5},{5,6},{6,7},{8,9},{9,10},{10,11},{11... | collective-permute-start | bytes 1179656 | tf_op jit(solution)/shard_map/while/body/eval_jaxpr/ppermute | solution.py:92
  3457.2 9.1 collective-permute-start
  (10 other events, 100.6 us)
Sparse Core Ops, SparseCore 0:
  3469.5 514.2 reduce-scatter.1
where the time goes:
time: 4030 us; the launch traced here: 3990 us
  local copies, waits for them, and re-layouts  1410 us (35%)
  matrix products  865 us (21%)
  waiting for transfers between devices  717 us (18%)
  starting transfers between devices  568 us (14%)
  other arithmetic  416 us (10%)
    ppermute x23, starting transfers between devices, step_body(): recv_act = lax.ppermute(hidden, 'pp', send_pairs)  568 us
    reduce_scatter x1, waiting for transfers between devices, stage_program(): x_out = lax.psum_scatter(last_only, 'pp', scatter_dimension=1, tiled=True)  497 us
    another operation x33, local copies, waits for them, and re-layouts  333 us
    dynamic_update_slice x16, local copies, waits for them, and re-layouts, run_patch(): lax.dynamic_update_slice(v_buf, v_fresh.reshape(1, batch_size, 1, patch_t...  332 us
    dynamic_update_slice x16, local copies, waits for them, and re-layouts, run_patch(): lax.dynamic_update_slice(k_buf, k_rot.reshape(1, batch_size, 1, patch_tok...  332 us
    dot_general x16, matrix products, run_patch(): jnp.einsum('btd,de->bte', h_mod, w_one[layer_idx], preferred_element_type...  240 us
    sub x16, matrix products, run_patch(): prob_bf = jax.nn.softmax(scores, axis=-1).astype(jnp.bfloat16)  231 us
    ppermute x23, waiting for transfers between devices, step_body(): recv_act = lax.ppermute(hidden, 'pp', send_pairs)  220 us
  transfers between devices with their start and end apart: 24, of which 24 were waited for; matrix products, arithmetic and copies ran while one was open for 2% of the time, Pallas kernels for 0%

commit v1 on v0

v1 whole, which is shorter than its diff:
```python
import functools
import math

import jax
import jax.numpy as jnp
from jax import lax
from jax.experimental import pallas as pl
from jax.experimental.pallas import tpu as pltpu
from jax.sharding import PartitionSpec as P

MESH = pl.DeviceIdType.MESH
F32 = jnp.float32
BF16 = jnp.bfloat16
LOG2E = 1.4426950408889634


def mm(a, b):
    return jnp.dot(a, b, preferred_element_type=F32)


def gelu(u):
    inner = u * (0.7978845608028654 + 0.035677408136300125 * (u * u))
    half = 0.5 * u
    return half + half * jnp.tanh(inner)


def block_kernel(dims, x_hbm, w1_hbm, w2_hbm, kp_hbm, vp_hbm, cos_hbm, sin_hbm, modp, b1, gains, ones,
                 xo_hbm, kn_hbm, vn_hbm,
                 w1, w2a, w2s, kbuf, vt, sbuf, qrhs, h, xs, snd, acc, attn, vst, tab,
                 w1_sem, wm_sem, w2a_sem, w2s_sem, kp_sem, vp_sem, x_sem, snd_sem, xo_sem, kn_sem, vn_sem, tab_sem, credit):
    stages, patches, tok, width, mlp, hd = dims
    seq = patches * tok
    pair = 2 * hd
    pairs = width // pair
    qkv = 3 * width
    mcol = mlp // pairs
    slots = w2s.shape[0]
    per = patches // stages
    expc = LOG2E / math.sqrt(hd)
    stage = lax.axis_index('pp') if stages > 1 else jnp.int32(0)
    last = stages - 1

    def w1_copy(j):
        cols = pl.ds(j * (qkv // 3), qkv // 3)
        return pltpu.make_async_copy(w1_hbm.at[:, cols], w1.at[:, cols], w1_sem.at[j])

    def wm_copy(i):
        cols = pl.ds(pl.multiple_of(qkv + i * mcol, mcol), mcol)
        return pltpu.make_async_copy(w1_hbm.at[:, cols], w1.at[:, cols], wm_sem.at[i])

    def w2s_copy(i, slot):
        return pltpu.make_async_copy(w2_hbm.at[pl.ds(pl.multiple_of(width + i * mcol, mcol), mcol), :], w2s.at[slot], w2s_sem.at[slot])

    w2a_copy = pltpu.make_async_copy(w2_hbm.at[pl.ds(0, width), :], w2a, w2a_sem)
    kp_copy = pltpu.make_async_copy(kp_hbm.at[pl.ds(tok, seq - tok), :], kbuf.at[pl.ds(tok, seq - tok), :], kp_sem)

    vrows = mcol
    vparts = seq // vrows

    def vp_copy(p):
        return pltpu.make_async_copy(vp_hbm.at[pl.ds(p * vrows, vrows), :], w2s.at[p % slots], vp_sem.at[p % slots])

    def x_copy(m, slot):
        return pltpu.make_async_copy(x_hbm.at[m], xs.at[slot], x_sem.at[slot])

    def tab_copies(m, slot):
        return (pltpu.make_async_copy(cos_hbm.at[m], tab.at[slot, 0], tab_sem.at[slot, 0]),
                pltpu.make_async_copy(sin_hbm.at[m], tab.at[slot, 1], tab_sem.at[slot, 1]))

    def kn_copy(m, slot):
        rows = pl.ds(pl.multiple_of(m * tok, tok), tok)
        return pltpu.make_async_copy(kbuf.at[rows, :], kn_hbm.at[rows, :], kn_sem.at[slot])

    def vn_copy(m, slot):
        rows = pl.ds(pl.multiple_of(m * tok, tok), tok)
        return pltpu.make_async_copy(vst.at[slot], vn_hbm.at[rows, :], vn_sem.at[slot])

    def send_copy(slot):
        return pltpu.make_async_remote_copy(
            src_ref=snd.at[slot], dst_ref=xs.at[slot], send_sem=snd_sem.at[slot], recv_sem=x_sem.at[slot],
            device_id={'pp': jnp.minimum(stage + 1, last)}, device_id_type=MESH)

    def give_copy(slot, owner, place):
        return pltpu.make_async_remote_copy(
            src_ref=snd.at[slot], dst_ref=xo_hbm.at[place], send_sem=snd_sem.at[slot], recv_sem=xo_sem.at[place],
            device_id={'pp': owner}, device_id_type=MESH)

    def keep_copy(slot, place):
        return pltpu.make_async_copy(snd.at[slot], xo_hbm.at[place], snd_sem.at[slot])

    if stages > 1:
        barrier = pltpu.get_barrier_semaphore()

        def greet(d, c):
            pl.semaphore_signal(barrier, inc=1, device_id={'pp': lax.rem(stage + d, stages)}, device_id_type=MESH)
            return c
        lax.fori_loop(1, stages, greet, 0)

    @pl.when(stage == 0)
    def _():
        x_copy(0, 0).start()
        x_copy(1, 1).start()
    for c in tab_copies(0, 0):
        c.start()
    for j in range(3):
        w1_copy(j).start()
    for p in range(slots):
        vp_copy(p).start()
    kp_copy.start()
    for i in range(pairs):
        wm_copy(i).start()
    w2a_copy.start()

    qrhs[...] = jnp.zeros_like(qrhs)
    if stages > 1:
        pl.semaphore_wait(barrier, stages - 1)

    def patch_step(m, carry):
        slot = lax.rem(m, 2)
        rows = pl.ds(pl.multiple_of(m * tok, tok), tok)
        x_copy(0, slot).wait()
        for c in tab_copies(0, slot):
            c.wait()

        @pl.when(m + 1 < patches)
        def _():
            for c in tab_copies(m + 1, 1 - slot):
                c.start()

        xv = xs[slot].astype(F32)
        cen = xv - jnp.mean(xv, axis=1, keepdims=True)
        nrm = cen * lax.rsqrt(jnp.mean(cen * cen, axis=1, keepdims=True) + 1e-6)
        h[...] = (nrm * modp[1:2, :] + modp[0:1, :]).astype(BF16)
        acc[...] = jnp.zeros_like(acc)

        @pl.when(m == 0)
        def _():
            for j in range(3):
                w1_copy(j).wait()

        @pl.when(m >= 2)
        def _():
            vn_copy(0, slot).wait()
            kn_copy(0, slot).wait()

        lane = lax.broadcasted_iota(jnp.int32, (tok, pair), 1)
        even = (lane % 2) == 0
        cos_t = tab[slot, 0]
        sin_t = tab[slot, 1]

        def head_norm(raw, ga, gb):
            r32 = raw.astype(F32)
            sq = r32 * r32
            hi = sq.astype(BF16)
            lo = (sq - hi.astype(F32)).astype(BF16)
            ssq = mm(hi, ones[...]) + mm(lo, ones[...])
            inv = lax.rsqrt(ssq * (1.0 / hd) + 1e-6)
            outs = []
            for t in range(2):
                part = r32[:, t * pair:(t + 1) * pair]
                other = jnp.where(even, pltpu.roll(part, pair - 1, 1), pltpu.roll(part, 1, 1))
                outs.append(((part * ga + other * gb) * inv[:, t * pair:(t + 1) * pair]).astype(BF16))
            return outs

        gq = cos_t * gains[0:1, :]
        gqs = sin_t * gains[1:2, :]
        gk = cos_t * gains[2:3, :]
        gks = sin_t * gains[3:4, :]
        blk = 2 * pair

        def qkv_step(j, c):
            def proj(base):
                cols = pl.ds(pl.multiple_of(base + j * blk, blk), blk)
                return (mm(h[...], w1[:, cols]) + b1[:, cols]).astype(BF16)
            raw_q = proj(0)
            raw_k = proj(width)
            raw_v = proj(2 * width)
            vst[slot, :, pl.ds(pl.multiple_of(j * blk, blk), blk)] = raw_v
            vt[pl.ds(pl.multiple_of(j * blk, blk), blk), rows] = raw_v.T
            q2 = head_norm(raw_q, gq, gqs)
            k2 = head_norm(raw_k, gk, gks)
            for t in range(2):
                qt = q2[t].T
                qrhs[2 * j + t, 0:hd, 0:tok] = qt[0:hd, :]
                qrhs[2 * j + t, hd:pair, tok:2 * tok] = qt[hd:pair, :]
                kbuf[rows, pl.ds(pl.multiple_of(j * blk + t * pair, pair), pair)] = k2[t]
            return c
        lax.fori_loop(0, width // blk, qkv_step, 0)

        kn_copy(m, slot).start()
        vn_copy(m, slot).start()

        @pl.when(m == 0)
        def _():
            for p in range(vparts):
                vp_copy(p).wait()

                def turn(d, c, p=p):
                    ds = pl.ds(pl.multiple_of(d * pair, pair), pair)
                    for t in range(vrows // tok):
                        if p * vrows + t * tok >= tok:
                            vt[ds, pl.ds(p * vrows + t * tok, tok)] = w2s[p % slots, pl.ds(t * tok, tok), ds].T
                    return c
                lax.fori_loop(0, pairs, turn, 0)
                if p + slots < vparts:
                    vp_copy(p + slots).start()
            for i in range(slots - 1):
                w2s_copy(i, i).start()
            kp_copy.wait()

        def pair_step(i, c):
            ws = lax.rem(i, slots)
            w2s_copy(0, ws).wait()

            @pl.when(m == 0)
            def _():
                wm_copy(i).wait()
            nxt = i + slots - 1

            @pl.when(jnp.logical_or(m + 1 < patches, nxt < pairs))
            def _():
                w2s_copy(lax.rem(nxt, pairs), lax.rem(nxt, slots)).start()
            lanes = pl.ds(pl.multiple_of(i * pair, pair), pair)
            rhs = qrhs[i]
            ck = 2 * tok
            top = None
            for b in range(seq // ck):
                s = mm(kbuf[b * ck:(b + 1) * ck, lanes], rhs)
                sbuf[b * ck:(b + 1) * ck, :] = s
                t8 = jnp.max(s.reshape(ck // 8, 8, 2 * tok), axis=0)
                top = t8 if top is None else jnp.maximum(top, t8)
            top = jnp.max(top, axis=0, keepdims=True)
            mcols = pl.ds(pl.multiple_of(qkv + i * mcol, mcol), mcol)
            up = (mm(h[...], w1[:, mcols]) + b1[:, mcols]).astype(BF16)
            act = gelu(up.astype(F32)).astype(BF16)
            acc[...] += mm(act, w2s[ws])
            tot = None
            out = None
            for b in range(seq // ck):
                e = jnp.exp2((sbuf[b * ck:(b + 1) * ck, :] - top) * expc)
                l8 = jnp.sum(e.reshape(ck // 8, 8, 2 * tok), axis=0)
                tot = l8 if tot is None else tot + l8
                o = mm(vt[lanes, b * ck:(b + 1) * ck], e.astype(BF16))
                out = o if out is None else out + o
            inv = 1.0 / jnp.sum(tot, axis=0, keepdims=True)
            both = jnp.concatenate([out[0:hd, 0:tok] * inv[:, 0:tok], out[hd:pair, tok:2 * tok] * inv[:, tok:2 * tok]], axis=0)
            attn[:, lanes] = both.astype(BF16).T
            return c
        lax.fori_loop(0, pairs, pair_step, 0)

        @pl.when(m == 0)
        def _():
            w2a_copy.wait()

        @pl.when(m >= 2)
        def _():
            if stages > 1:
                @pl.when(stage < last)
                def _():
                    send_copy(slot).wait_send()
                    pl.semaphore_wait(credit, 1)

                @pl.when(stage == last)
                def _():
                    keep_copy(slot, 0).wait()
            else:
                keep_copy(slot, 0).wait()

        for n in range(width // blk):
            cols = slice(n * blk, (n + 1) * blk)
            o = mm(attn[...], w2a[:, cols]) + acc[:, cols] + modp[3:4, cols]
            snd[slot, :, cols] = (xs[slot, :, cols].astype(F32) + modp[2:3, cols] * o).astype(BF16)

        if stages > 1:
            @pl.when(stage < last)
            def _():
                send_copy(slot).start()

            @pl.when(stage == last)
            def _():
                owner = m // per

                @pl.when(owner < last)
                def _():
                    give_copy(slot, jnp.minimum(owner, last - 1), lax.rem(m, per)).start()

                @pl.when(owner == last)
                def _():
                    keep_copy(slot, lax.rem(m, per)).start()

            @pl.when(jnp.logical_and(stage > 0, m + 2 < patches))
            def _():
                pl.semaphore_signal(credit, inc=1, device_id={'pp': jnp.maximum(stage - 1, 0)}, device_id_type=MESH)
        else:
            keep_copy(slot, m).start()

        @pl.when(jnp.logical_and(stage == 0, m + 2 < patches))
        def _():
            x_copy(m + 2, slot).start()
        return carry

    lax.fori_loop(0, patches, patch_step, 0)

    for slot in range(2):
        kn_copy(0, slot).wait()
        vn_copy(0, slot).wait()
        if stages > 1:
            @pl.when(stage < last)
            def _():
                send_copy(slot).wait_send()

            @pl.when(stage == last)
            def _():
                keep_copy(slot, 0).wait()
        else:
            keep_copy(slot, 0).wait()
    if stages > 1:
        @pl.when(stage < last)
        def _():
            for place in range(per):
                give_copy(0, 0, place).wait_recv()


def rope_rows(pos_ids, head_dim):
    axis_zero = head_dim // 8
    axis_rest = (head_dim - axis_zero) // 2
    pieces = []
    for axis_idx, axis_dim in enumerate((axis_zero, axis_rest, head_dim - axis_zero - axis_rest)):
        axis_freqs = 1.0 / (10000.0 ** (jnp.arange(0, axis_dim, 2, dtype=F32) / axis_dim))
        pieces.append(pos_ids[..., axis_idx:axis_idx + 1].astype(F32) * axis_freqs)
    angles = jnp.concatenate(pieces, axis=-1)
    cos = jnp.repeat(jnp.cos(angles), 2, axis=-1)
    sin = jnp.sin(angles)
    sin = jnp.stack([-sin, sin], axis=-1).reshape(cos.shape)
    return jnp.concatenate([cos, cos], axis=-1), jnp.concatenate([sin, sin], axis=-1)


def make_stage(stages):
    def stage_program(x_in, cond_vec, pos_ids, w_mod, b_mod, w_one, b_one, qk_scale, w_two, b_two, k_prev, v_prev):
        batch, patches, tok, width = x_in.shape
        hd = qk_scale.shape[-1]
        mlp = w_two.shape[1] - width
        seq = patches * tok
        pair = 2 * hd
        pairs = width // pair
        mcol = mlp // pairs
        per = patches // stages
        cond_act = jax.nn.silu(cond_vec.astype(F32)).astype(BF16)
        mod = jnp.dot(cond_act, w_mod[0], preferred_element_type=F32)[0] + b_mod[0].astype(F32)
        modp = jnp.stack([mod[:width], 1.0 + mod[width:2 * width], mod[2 * width:], b_two[0].astype(F32)])
        cos_t, sin_t = rope_rows(pos_ids, hd)
        g = qk_scale[0].astype(F32)
        gsw = g.reshape(2, hd // 2, 2)[:, :, ::-1].reshape(2, hd)
        gains = jnp.stack([g[0], gsw[0], g[1], gsw[1]])
        gains = jnp.concatenate([gains, gains], axis=1)
        head_id = jnp.arange(2 * pair) // hd
        ones = (head_id[:, None] == head_id[None, :]).astype(BF16)
        hbm = functools.partial(pltpu.with_memory_space_constraint, memory_space=pltpu.HBM)
        dims = (stages, patches, tok, width, mlp, hd)
        out_patches = per
        x_out, k_new, v_new = pl.pallas_call(
            functools.partial(block_kernel, dims),
            out_shape=(jax.ShapeDtypeStruct((out_patches, tok, width), BF16),
                       jax.ShapeDtypeStruct((seq, width), BF16), jax.ShapeDtypeStruct((seq, width), BF16)),
            in_specs=[pl.BlockSpec(memory_space=pltpu.HBM)] * 7 + [pl.BlockSpec(memory_space=pltpu.VMEM)] * 4,
            out_specs=(pl.BlockSpec(memory_space=pltpu.HBM),) * 3,
            scratch_shapes=[
                pltpu.VMEM((width, 3 * width + mlp), BF16),
                pltpu.VMEM((width, width), BF16),
                pltpu.VMEM((3, mcol, width), BF16),
                pltpu.VMEM((seq, width), BF16),
                pltpu.VMEM((width, seq), BF16),
                pltpu.VMEM((seq, 2 * tok), F32),
                pltpu.VMEM((pairs, pair, 2 * tok), BF16),
                pltpu.VMEM((tok, width), BF16),
                pltpu.VMEM((2, tok, width), BF16),
                pltpu.VMEM((2, tok, width), BF16),
                pltpu.VMEM((tok, width), F32),
                pltpu.VMEM((tok, width), BF16),
                pltpu.VMEM((2, tok, width), BF16),
                pltpu.VMEM((2, 2, tok, pair), F32),
                pltpu.SemaphoreType.DMA((3,)),
                pltpu.SemaphoreType.DMA((pairs,)),
                pltpu.SemaphoreType.DMA,
                pltpu.SemaphoreType.DMA((3,)),
                pltpu.SemaphoreType.DMA,
                pltpu.SemaphoreType.DMA((3,)),
                pltpu.SemaphoreType.DMA((2,)),
                pltpu.SemaphoreType.DMA((2,)),
                pltpu.SemaphoreType.DMA((per,)),
                pltpu.SemaphoreType.DMA((2,)),
                pltpu.SemaphoreType.DMA((2,)),
                pltpu.SemaphoreType.DMA((2, 2)),
                pltpu.SemaphoreType.REGULAR,
            ],
            compiler_params=pltpu.CompilerParams(
                vmem_limit_bytes=67043328, **(dict(collective_id=0, has_side_effects=True) if stages > 1 else {})),
            name='blocks',
        )(hbm(x_in[0]), hbm(w_one[0]), hbm(w_two[0]), hbm(k_prev.reshape(seq, width)), hbm(v_prev.reshape(seq, width)),
          hbm(cos_t), hbm(sin_t), modp, b_one.astype(F32), gains, ones)
        return x_out[None], k_new.reshape(k_prev.shape), v_new.reshape(v_prev.shape)
    return stage_program


def solution(mesh):
    stages = mesh.shape['pp']
    return jax.shard_map(
        make_stage(stages), mesh=mesh,
        in_specs=(P('dp'), P('dp'), P(), P('pp'), P('pp'), P('pp'), P('pp'), P('pp'), P('pp'), P('pp'), P('pp', 'dp'), P('pp', 'dp')),
        out_specs=(P('dp', 'pp'), P('pp', 'dp'), P('pp', 'dp')),
        check_vma=False)
```

time: 4030 us -> 632 us (0.16)
  the two profiles are of different devices: /device:TPU:81 before, /device:TPU:87 now
where the time goes in v1:
time: 632 us
  Pallas kernels  604 us (96%)
  local copies, waits for them, and re-layouts  12.5 us (2%)
  other arithmetic  7.99 us (1%)
  matrix products  7.01 us (1%)
    pallas_call x1, Pallas kernels, stage_program(): pl.pallas_call(functools.partial(block_kernel, dims), out_shape=(jax.Shap...  604 us

profile of v1, /device:TPU:87, one launch (start us, length us, event | category | flops | bytes accessed | tf_op | source)
XLA Modules:
  0.0 632.0 jit_solution(13544332899958140984)
XLA Ops:
  0.7 0.7 convert_element_type.46
  1.3 0.7 convert_element_type.44
  2.0 0.1 slice.58
  2.1 0.1 slice.59
  2.2 0.1 slice.60
  2.3 0.1 slice.63
  2.4 0.1 slice.64
  2.5 0.1 slice.65
  2.6 0.7 maximum_maximum_fusion.gains
  3.3 0.0 copy-start.2
  3.3 0.0 copy-start.1
  3.3 0.0 copy-start
  3.3 7.0 %fusion.2 = f32[4608]{0:T(1024)S(1)} fusion(bf16[1,1536,4608]{2,1,0:T(8,128)(2,1)} %param.15, bf16[1,1536]{1,0:T(2,128)(2,1)} %param.13), kind=kOutput, calls=%fused_computation.2 | convolution fusion | flops 14164992 | bytes 14177280 | tf_op jit(solution)/shard_map/dot_general | solution.py:349
  10.3 0.0 copy-done.2
  10.3 0.1 convert_reduce_fusion
  10.4 0.6 pad_maximum_fusion.3.modp
  11.1 0.0 copy-done.1
  11.1 0.0 copy-done
  11.1 0.7 convert_element_type.45.b1
  11.7 0.1 fusion.7
  11.8 0.8 compare_convert_fusion.ones
  12.6 0.1 fusion.5
  12.7 0.8 maximum_cosine_fusion
  13.6 0.9 fusion.15
  14.5 0.4 copy.20
  14.8 0.4 copy.17
  15.2 1.9 pad_maximum_fusion
  17.1 603.8 %blocks.1 = (bf16[2,128,1536]{2,1,0:T(8,128)(2,1)}, bf16[2048,1536]{1,0:T(8,128)(2,1)}, bf16[2048,1536]{1,0:T(8,128)(2,1)}) custom-call(bf16[16,128,1536]{2,1,0:T(8,128)(2,1)} %bitcast.38, bf16[1536,10752]{1,0:T(8,128)(2,1)} %bitcast.36, bf16[7680,1536]{1,0:T(8,128)(2,1)} %bitcast.37, bf16[2048,1536]{1,0:T(8,128)(2,1)} %bitcast.39, ...), custom_call_target="tpu_custom_call" | custom-call | tf_op jit(solution)/shard_map/blocks/pallas_call | solution.py:361
  620.9 0.0 slice-start
  620.9 2.2 copy.25
  623.1 0.0 slice-start.1
  623.1 6.2 copy.26
  629.3 0.0 slice-done
  629.3 0.0 slice-done.1
  629.3 2.7 copy.27
  (13 shorter events, 0.2 us)
Async XLA Ops:
  3.3 7.0 %copy-start.2 = (bf16[1,4608]{1,0:T(2,128)(2,1)S(1)}, bf16[1,4608]{1,0:T(2,128)(2,1)}, u32[]{:S(2)}) copy-start(bf16[1,4608]{1,0:T(2,128)(2,1)} %param.16) | copy-start | bytes 27652
  3.3 7.8 %copy-start.1 = (s32[16,128,3]{1,0,2:T(8,128)S(1)}, s32[16,128,3]{1,0,2:T(8,128)}, u32[]{:S(2)}) copy-start(s32[16,128,3]{1,0,2:T(8,128)} %param.14) | copy-start | bytes 73732
  3.3 7.8 %copy-start = (bf16[1,10752]{1,0:T(2,128)(2,1)S(1)}, bf16[1,10752]{1,0:T(2,128)(2,1)}, u32[]{:S(2)}) copy-start(bf16[1,10752]{1,0:T(2,128)(2,1)} %param.18) | copy-start | bytes 64516
  620.9 8.4 %slice-start = ((s8[6291456]{0:T(1024)(128)(4,1)}), s8[4194304]{0:T(1024)(128)(4,1)S(1)}, s32[]{:S(2)}) async-start(s8[6291456]{0:T(1024)(128)(4,1)} %bitcast.41), calls=%async_computation | async-start | bytes 8388608
  623.1 6.2 slice-start.1
